TPU v7x, 32 devices: a whole 2x2x4 slice. The times are simulated.
32 devices in a mesh: shots: 1, gx: 32 (over z, y, x, core), gy: 1.
Axes of the slice: x: 2, y: 2, z: 4, core: 2. Of those that a mesh axis runs over, the one named last changes fastest.
Arguments:
- pressure: float32 [128, 256, 128], P(None, ('shots', 'gx'), 'gy'), may hold values from -6 to 6
- pressure_prior: float32 [128, 256, 128], P(None, ('shots', 'gx'), 'gy'), may hold values from -6 to 6
- courant_square: bfloat16 [128, 256, 128], P(None, 'gx', 'gy'), may hold values from 0.049804688 to 0.1796875
- wavelet: float32 [16], P('shots'), may hold values from -4 to 4
- delay_steps: int32 [256, 128], P(('shots', 'gx'), 'gy'), may hold values from 0 to 7
- source_depth: int32 [256, 128], P(('shots', 'gx'), 'gy'), may hold values from 4 to 31
- receiver_depth: int32 [256, 128], P(('shots', 'gx'), 'gy'), may hold values from 0 to 31
- receiver_field: float32 [128, 256, 128], P(None, ('shots', 'gx'), 'gy'), may hold values from -6 to 6
Outputs:
- pressure_final: float32 [128, 256, 128], P(None, ('shots', 'gx'), 'gy')
- image: float32 [128, 256, 128], P('gx', 'shots', 'gy')
All inputs are finite; a program needn't handle non-finite values.
Results may differ from a plain program's by a relative error of at most 0.00035.
Values sent between devices are 32-bit elements; how exact they have to be, the bound alone decides.
A program may use at most 64 MiB of HBM per device.

v0:
```python
import functools

import jax
import jax.numpy as jnp
from jax import lax
from jax.experimental import pallas as pl
from jax.experimental.pallas import tpu as pltpu
from jax.sharding import PartitionSpec as P

STEPS = 8
REACH = 4
CENTER = -205.0 / 72.0
COEFS = (1.6, -0.2, 8.0 / 315.0, -1.0 / 560.0)
CHUNKS = 4
GROUP = 8


def kernel(
    nx,
    ny,
    pressure,
    prior,
    courant,
    wavelet,
    delay,
    sdepth,
    rdepth,
    receiver,
    final,
    image,
    field,
    side,
    prior_v,
    courant_v,
    receiver_v,
    amp,
    product,
    slab,
    local_sem,
    send_sem,
    recv_sem,
    side_send,
    side_recv,
    out_sem,
    img_send,
    img_recv,
):
    depth, width, length = pressure.shape
    rows = depth // CHUNKS
    slab_depth = depth // nx
    me = lax.axis_index("gx")
    mine = lax.axis_index("gy")

    local = [
        pltpu.make_async_copy(
            pressure, field.at[0, pl.ds(REACH, depth), pl.ds(REACH, width), :], local_sem.at[0]
        ),
        pltpu.make_async_copy(prior, prior_v, local_sem.at[1]),
        pltpu.make_async_copy(courant, courant_v, local_sem.at[2]),
        pltpu.make_async_copy(receiver, receiver_v, local_sem.at[3]),
    ]
    for copy in local:
        copy.start()

    barrier = pltpu.get_barrier_semaphore()
    for j in range(1, nx):
        pl.semaphore_signal(
            barrier,
            inc=1,
            device_id={"gx": lax.rem(me + j, nx)},
            device_id_type=pl.DeviceIdType.MESH,
        )
    for j in range(1, ny):
        pl.semaphore_signal(
            barrier,
            inc=1,
            device_id={"gy": lax.rem(mine + j, ny)},
            device_id_type=pl.DeviceIdType.MESH,
        )

    rim = jnp.zeros((REACH, width + 2 * REACH, length), jnp.float32)
    for t in range(STEPS):
        field[t, pl.ds(0, REACH), :, :] = rim
        field[t, pl.ds(REACH + depth, REACH), :, :] = rim

    def clear(at):
        def one(i, carry):
            t = i // CHUNKS
            c = i % CHUNKS
            field[t, pl.ds(REACH + c * rows, rows), pl.ds(at, REACH), :] = jnp.zeros(
                (rows, REACH, length), jnp.float32
            )
            return carry

        lax.fori_loop(0, STEPS * CHUNKS, one, 0)

    @pl.when(me == 0)
    def _():
        clear(0)

    @pl.when(me == nx - 1)
    def _():
        clear(REACH + width)

    if ny > 1:

        def clear_side(k):
            def one(i, carry):
                t = i // CHUNKS
                c = i % CHUNKS
                side[t, k, pl.ds(c * rows, rows), :, :] = jnp.zeros(
                    (rows, width, length), jnp.float32
                )
                return carry

            lax.fori_loop(0, STEPS * CHUNKS, one, 0)

        @pl.when(mine == 0)
        def _():
            clear_side(0)

        @pl.when(mine == ny - 1)
        def _():
            clear_side(1)

    late = delay[...]
    for t in range(STEPS):
        total = jnp.zeros((width, length), jnp.float32)
        for pick in range(wavelet.shape[0]):
            total = total + jnp.where(late + t == pick, wavelet[pick], 0.0)
        amp[t] = total

    if nx + ny > 2:
        pl.semaphore_wait(barrier, nx + ny - 2)

    def span(c):
        return pl.ds(REACH + c * rows, rows)

    def face(t, c, way):
        source = REACH + width - REACH if way == 0 else REACH
        target = 0 if way == 0 else REACH + width
        peer = lax.rem(me + 1, nx) if way == 0 else lax.rem(me + nx - 1, nx)
        return pltpu.make_async_remote_copy(
            src_ref=field.at[t, span(c), pl.ds(source, REACH), :],
            dst_ref=field.at[t, span(c), pl.ds(target, REACH), :],
            send_sem=send_sem.at[t, c, way],
            recv_sem=recv_sem.at[t, c, way],
            device_id={"gx": peer},
            device_id_type=pl.DeviceIdType.MESH,
        )

    def flank(t, c, way):
        peer = lax.rem(mine + 1, ny) if way == 0 else lax.rem(mine + ny - 1, ny)
        return pltpu.make_async_remote_copy(
            src_ref=field.at[t, span(c), pl.ds(REACH, width), :],
            dst_ref=side.at[t, way, pl.ds(c * rows, rows), :, :],
            send_sem=side_send.at[t, c, way],
            recv_sem=side_recv.at[t, c, way],
            device_id={"gy": peer},
            device_id_type=pl.DeviceIdType.MESH,
        )

    def each_face(t, c, act, sending):
        lower, upper = (me > 0, me < nx - 1)
        if nx > 1:
            for way in (0, 1):
                there = upper if (way == 0) == sending else lower

                @pl.when(there)
                def _():
                    act(face(t, c, way))

        if ny > 1:
            for way in (0, 1):
                there = mine < ny - 1 if (way == 0) == sending else mine > 0

                @pl.when(there)
                def _():
                    act(flank(t, c, way))

    def send(t, c):
        each_face(t, c, lambda copy: copy.start(), True)

    def sent(t, c):
        each_face(t, c, lambda copy: copy.wait_send(), True)

    def arrived(t, c):
        each_face(t, c, lambda copy: copy.wait_recv(), False)

    local[0].wait()
    for c in range(CHUNKS):
        send(0, c)
    local[1].wait()
    local[2].wait()

    lanes = lax.broadcasted_iota(jnp.int32, (width, length), 1)
    ahead = [jnp.where(lanes < length - k, COEFS[k - 1], 0.0) for k in range(1, REACH + 1)]
    behind = [jnp.where(lanes >= k, COEFS[k - 1], 0.0) for k in range(1, REACH + 1)]
    origin = sdepth[...]

    def advance(t, z, old):
        own = pl.ds(REACH, width)
        v = field[t, pl.ds(REACH + z, GROUP), own, :]
        total = (3.0 * CENTER) * v
        for k in range(1, REACH + 1):
            near = (
                field[t, pl.ds(REACH + z + k, GROUP), own, :]
                + field[t, pl.ds(REACH + z - k, GROUP), own, :]
            )
            near = near + (
                field[t, pl.ds(REACH + z, GROUP), pl.ds(REACH + k, width), :]
                + field[t, pl.ds(REACH + z, GROUP), pl.ds(REACH - k, width), :]
            )
            total = total + COEFS[k - 1] * near
            up = pltpu.roll(v, length - k, 2)
            down = pltpu.roll(v, k, 2)
            if ny > 1:
                low = pltpu.roll(side[t, 0, pl.ds(z, GROUP), :, :], k, 2)
                high = pltpu.roll(side[t, 1, pl.ds(z, GROUP), :, :], length - k, 2)
                up = jnp.where((lanes < length - k)[None], up, high)
                down = jnp.where((lanes >= k)[None], down, low)
                total = total + COEFS[k - 1] * (up + down)
            else:
                total = total + ahead[k - 1][None] * up + behind[k - 1][None] * down
        strength = courant_v[pl.ds(z, GROUP), :, :].astype(jnp.float32)
        levels = lax.broadcasted_iota(jnp.int32, (GROUP, width, length), 0) + z
        shot = jnp.where(levels == origin[None], amp[t][None], 0.0)
        return 2.0 * v - old + strength * total + shot

    def first_chunk(c, carry):
        arrived(0, c)

        def group(g, inner):
            z = c * rows + g * GROUP
            new = advance(0, z, prior_v[pl.ds(z, GROUP), :, :])
            field[1, pl.ds(REACH + z, GROUP), pl.ds(REACH, width), :] = new
            return inner

        lax.fori_loop(0, rows // GROUP, group, 0)
        send(1, c)
        return carry

    lax.fori_loop(0, CHUNKS, first_chunk, 0)

    def step(i, carry):
        t = i // CHUNKS
        c = i % CHUNKS
        arrived(t, c)

        def group(g, inner):
            z = c * rows + g * GROUP
            old = field[t - 1, pl.ds(REACH + z, GROUP), pl.ds(REACH, width), :]
            new = advance(t, z, old)
            field[t + 1, pl.ds(REACH + z, GROUP), pl.ds(REACH, width), :] = new
            return inner

        lax.fori_loop(0, rows // GROUP, group, 0)

        @pl.when(t < STEPS - 1)
        def _():
            send(t + 1, c)

        return carry

    lax.fori_loop(CHUNKS, STEPS * CHUNKS, step, 0)

    done = pltpu.make_async_copy(
        field.at[STEPS, pl.ds(REACH, depth), pl.ds(REACH, width), :], final, out_sem.at[0]
    )
    done.start()

    local[3].wait()
    ground = rdepth[...]
    product[pl.ds(0, 1), :, :] = jnp.zeros((1, width, length), jnp.float32)
    product[pl.ds(depth + 1, 1), :, :] = jnp.zeros((1, width, length), jnp.float32)

    def multiply(g, carry):
        z = g * GROUP
        levels = lax.broadcasted_iota(jnp.int32, (GROUP, width, length), 0) + z
        masked = jnp.where(levels >= ground[None], receiver_v[pl.ds(z, GROUP), :, :], 0.0)
        product[pl.ds(1 + z, GROUP), :, :] = (
            field[STEPS, pl.ds(REACH + z, GROUP), pl.ds(REACH, width), :] * masked
        )
        return carry

    lax.fori_loop(0, depth // GROUP, multiply, 0)

    def landing(who):
        return image.at[:, pl.ds(pl.multiple_of(who * width, width), width), :]

    def piece(peer):
        return pltpu.make_async_remote_copy(
            src_ref=slab.at[pl.ds(peer * slab_depth, slab_depth), :, :],
            dst_ref=landing(me),
            send_sem=img_send.at[peer],
            recv_sem=img_recv.at[me],
            device_id={"gx": peer},
            device_id_type=pl.DeviceIdType.MESH,
        )

    def kept():
        return pltpu.make_async_copy(
            slab.at[pl.ds(me * slab_depth, slab_depth), :, :], landing(me), out_sem.at[1]
        )

    def filtered(peer):
        z = peer * slab_depth
        slab[pl.ds(z, slab_depth), :, :] = (
            2.0 * product[pl.ds(1 + z, slab_depth), :, :]
            - product[pl.ds(z, slab_depth), :, :]
            - product[pl.ds(2 + z, slab_depth), :, :]
        )

    def ship(j, carry):
        peer = lax.rem(me + j, nx)
        filtered(peer)
        piece(peer).start()
        return carry

    lax.fori_loop(1, nx, ship, 0)
    filtered(me)
    kept().start()

    def drain(i, carry):
        sent(i // CHUNKS, i % CHUNKS)
        return carry

    lax.fori_loop(0, STEPS * CHUNKS, drain, 0)

    def finish(j, carry):
        peer = lax.rem(me + j, nx)
        piece(peer).wait_send()
        came = lax.rem(me + nx - j, nx)
        pltpu.make_async_remote_copy(
            src_ref=slab.at[pl.ds(me * slab_depth, slab_depth), :, :],
            dst_ref=landing(came),
            send_sem=img_send.at[came],
            recv_sem=img_recv.at[came],
            device_id={"gx": came},
            device_id_type=pl.DeviceIdType.MESH,
        ).wait_recv()
        return carry

    lax.fori_loop(1, nx, finish, 0)
    kept().wait()
    done.wait()


def solution(mesh):
    nx, ny = mesh.shape["gx"], mesh.shape["gy"]

    def shards(
        pressure, prior, courant, wavelet, delay, sdepth, rdepth, receiver
    ):
        depth, width, length = pressure.shape
        hbm = pl.BlockSpec(memory_space=pl.ANY)
        vmem = pl.BlockSpec(memory_space=pltpu.VMEM)
        smem = pl.BlockSpec(memory_space=pltpu.SMEM)
        flat = (depth, width, length)
        sides = (STEPS, 2, depth, width, length) if ny > 1 else (1, 1, 1, width, length)
        return pl.pallas_call(
            functools.partial(kernel, nx, ny),
            out_shape=(
                jax.ShapeDtypeStruct(flat, jnp.float32),
                jax.ShapeDtypeStruct((depth // nx, width * nx, length), jnp.float32),
            ),
            in_specs=[hbm, hbm, hbm, smem, vmem, vmem, vmem, hbm],
            out_specs=(hbm, hbm),
            scratch_shapes=[
                pltpu.VMEM((STEPS + 1, depth + 2 * REACH, width + 2 * REACH, length), jnp.float32),
                pltpu.VMEM(sides, jnp.float32),
                pltpu.VMEM(flat, jnp.float32),
                pltpu.VMEM(flat, jnp.bfloat16),
                pltpu.VMEM(flat, jnp.float32),
                pltpu.VMEM((STEPS, width, length), jnp.float32),
                pltpu.VMEM((depth + 2, width, length), jnp.float32),
                pltpu.VMEM(flat, jnp.float32),
                pltpu.SemaphoreType.DMA((4,)),
                pltpu.SemaphoreType.DMA((STEPS, CHUNKS, 2)),
                pltpu.SemaphoreType.DMA((STEPS, CHUNKS, 2)),
                pltpu.SemaphoreType.DMA((STEPS, CHUNKS, 2)),
                pltpu.SemaphoreType.DMA((STEPS, CHUNKS, 2)),
                pltpu.SemaphoreType.DMA((2,)),
                pltpu.SemaphoreType.DMA((nx,)),
                pltpu.SemaphoreType.DMA((nx,)),
            ],
            compiler_params=pltpu.CompilerParams(
                collective_id=0, has_side_effects=True, vmem_limit_bytes=48 * 1024 * 1024
            ),
        )(pressure, prior, courant, wavelet, delay, sdepth, rdepth, receiver)

    in_specs = (
        P(None, ("shots", "gx"), "gy"),
        P(None, ("shots", "gx"), "gy"),
        P(None, "gx", "gy"),
        P("shots"),
        P(("shots", "gx"), "gy"),
        P(("shots", "gx"), "gy"),
        P(("shots", "gx"), "gy"),
        P(None, ("shots", "gx"), "gy"),
    )
    out_specs = (P(None, ("shots", "gx"), "gy"), P("gx", "shots", "gy"))
    return jax.shard_map(shards, mesh=mesh, in_specs=in_specs, out_specs=out_specs, check_vma=False)
```

profile of v0, /device:TPU:29, one launch (start us, length us, event | category | flops | bytes accessed | tf_op | source)
XLA Modules:
  0.0 77.9 jit_solution(10421258351648389001)
XLA Ops:
  0.6 0.0 copy-start
  0.6 1.0 %copy-done = f32[128,8,128]{2,1,0:T(8,128)S(1)} copy-done((f32[128,8,128]{2,1,0:T(8,128)S(1)}, f32[128,8,128]{2,1,0:T(8,128)}, u32[]{:S(2)}) %copy-start) | copy-done | bytes 524312
  1.7 0.0 copy-start.1
  1.7 1.0 %copy-done.1 = f32[128,8,128]{2,1,0:T(8,128)S(1)} copy-done((f32[128,8,128]{2,1,0:T(8,128)S(1)}, f32[128,8,128]{2,1,0:T(8,128)}, u32[]{:S(2)}) %copy-start.1) | copy-done | bytes 524312
  2.7 0.0 copy-start.2
  2.7 1.0 %copy-done.2 = f32[128,8,128]{2,1,0:T(8,128)S(1)} copy-done((f32[128,8,128]{2,1,0:T(8,128)S(1)}, f32[128,8,128]{2,1,0:T(8,128)}, u32[]{:S(2)}) %copy-start.2) | copy-done | bytes 524312
  3.8 0.0 copy-start.3
  3.8 0.9 %copy-done.3 = bf16[128,8,128]{2,1,0:T(8,128)(2,1)S(1)} copy-done((bf16[128,8,128]{2,1,0:T(8,128)(2,1)S(1)}, bf16[128,8,128]{2,1,0:T(8,128)(2,1)}, u32[]{:S(2)}) %copy-start.3) | copy-done | bytes 262168
  4.7 0.0 copy-start.4
  4.7 0.7 copy-done.4
  5.4 0.0 copy-start.5
  5.4 0.7 copy-done.5
  6.1 0.0 copy-start.6
  6.1 0.7 copy-done.6
  6.8 0.0 copy-start.7
  6.8 0.7 copy-done.7
  7.4 68.8 %shard_map.95 = (f32[128,8,128]{2,1,0:T(8,128)S(1)}, f32[4,256,128]{2,1,0:T(8,128)S(1)}) custom-call(f32[128,8,128]{2,1,0:T(8,128)S(1)} %copy-done, f32[128,8,128]{2,1,0:T(8,128)S(1)} %copy-done.1, bf16[128,8,128]{2,1,0:T(8,128)(2,1)S(1)} %copy-done.3, f32[16]{0:T(128)S(1)} %copy-done.7, s32[8,128]{1,0:T(8,128)S(1)} %copy-done.4, s32[8,128]{1,0:T(8,128)S(1)} %copy-done.5, ...), custom_call_target="tpu_custom_call" | custom-call | tf_op jit(solution)/shard_map/pallas_call | solution.py:361
  76.3 0.8 %copy.12 = f32[128,8,128]{2,1,0:T(8,128)} copy(f32[128,8,128]{2,1,0:T(8,128)S(1)} %get-tuple-element.4) | data formatting | bytes 1048576
  77.1 0.8 %copy.13 = f32[4,256,128]{2,1,0:T(8,128)} copy(f32[4,256,128]{2,1,0:T(8,128)S(1)} %get-tuple-element.5) | data formatting | bytes 1048576
Async XLA Ops:
  0.6 1.0 %copy-start = (f32[128,8,128]{2,1,0:T(8,128)S(1)}, f32[128,8,128]{2,1,0:T(8,128)}, u32[]{:S(2)}) copy-start(f32[128,8,128]{2,1,0:T(8,128)} %pressure.1) | copy-start | bytes 1572868
  1.7 1.0 %copy-start.1 = (f32[128,8,128]{2,1,0:T(8,128)S(1)}, f32[128,8,128]{2,1,0:T(8,128)}, u32[]{:S(2)}) copy-start(f32[128,8,128]{2,1,0:T(8,128)} %prior.1) | copy-start | bytes 1572868
  2.7 1.0 %copy-start.2 = (f32[128,8,128]{2,1,0:T(8,128)S(1)}, f32[128,8,128]{2,1,0:T(8,128)}, u32[]{:S(2)}) copy-start(f32[128,8,128]{2,1,0:T(8,128)} %receiver.1) | copy-start | bytes 1572868
  3.8 0.9 %copy-start.3 = (bf16[128,8,128]{2,1,0:T(8,128)(2,1)S(1)}, bf16[128,8,128]{2,1,0:T(8,128)(2,1)}, u32[]{:S(2)}) copy-start(bf16[128,8,128]{2,1,0:T(8,128)(2,1)} %courant.1) | copy-start | bytes 786436
  4.7 0.7 copy-start.4
  5.4 0.7 copy-start.5
  6.1 0.7 copy-start.6
  6.8 0.7 copy-start.7
where the time goes:
time: 78.2 us; the launch traced here: 77.9 us
  Pallas kernels  68.8 us (88%)
  local copies, waits for them, and re-layouts  8.37 us (11%)
    pallas_call x1, Pallas kernels, shards(): pl.pallas_call(functools.partial(kernel, nx, ny), out_shape=(jax.ShapeDty...  68.8 us
    unnamed x18, local copies, waits for them, and re-layouts  8.37 us

commit v1 on v0

--- a/solution.py
+++ b/solution.py
@@ -36,6 +36,11 @@
     amp,
     product,
     slab,
+    weights,
+    wave_v,
+    delay_v,
+    sdepth_v,
+    rdepth_v,
     local_sem,
     send_sem,
     recv_sem,
@@ -58,6 +63,10 @@
         pltpu.make_async_copy(prior, prior_v, local_sem.at[1]),
         pltpu.make_async_copy(courant, courant_v, local_sem.at[2]),
         pltpu.make_async_copy(receiver, receiver_v, local_sem.at[3]),
+        pltpu.make_async_copy(wavelet, wave_v, local_sem.at[4]),
+        pltpu.make_async_copy(delay, delay_v, local_sem.at[5]),
+        pltpu.make_async_copy(sdepth, sdepth_v, local_sem.at[6]),
+        pltpu.make_async_copy(rdepth, rdepth_v, local_sem.at[7]),
     ]
     for copy in local:
         copy.start()
@@ -123,11 +132,13 @@
         def _():
             clear_side(1)
 
-    late = delay[...]
+    local[4].wait()
+    local[5].wait()
+    late = delay_v[...]
     for t in range(STEPS):
         total = jnp.zeros((width, length), jnp.float32)
         for pick in range(wavelet.shape[0]):
-            total = total + jnp.where(late + t == pick, wavelet[pick], 0.0)
+            total = total + jnp.where(late + t == pick, wave_v[pick], 0.0)
         amp[t] = total
 
     if nx + ny > 2:
@@ -194,14 +205,37 @@
     local[2].wait()
 
     lanes = lax.broadcasted_iota(jnp.int32, (width, length), 1)
-    ahead = [jnp.where(lanes < length - k, COEFS[k - 1], 0.0) for k in range(1, REACH + 1)]
-    behind = [jnp.where(lanes >= k, COEFS[k - 1], 0.0) for k in range(1, REACH + 1)]
-    origin = sdepth[...]
+    start = lax.broadcasted_iota(jnp.int32, (length, length), 0)
+    gap = jnp.abs(start - lax.broadcasted_iota(jnp.int32, (length, length), 1))
+    band = jnp.where(gap == 0, 3.0 * CENTER, 0.0)
+    for k in range(1, REACH + 1):
+        band = jnp.where(gap == k, COEFS[k - 1], band)
+    band_high = band.astype(jnp.bfloat16)
+    band_low = (band - band_high.astype(jnp.float32)).astype(jnp.bfloat16)
+    weights[...] = jnp.concatenate(
+        [
+            jnp.concatenate([band_high, band_low], axis=1),
+            jnp.concatenate([band_high, jnp.zeros_like(band_low)], axis=1),
+        ],
+        axis=0,
+    )
+
+    def along(v):
+        tall = v.reshape(GROUP * width, length)
+        high = tall.astype(jnp.bfloat16)
+        low = (tall - high.astype(jnp.float32)).astype(jnp.bfloat16)
+        both = jnp.dot(
+            jnp.concatenate([high, low], axis=1), weights[...], preferred_element_type=jnp.float32
+        )
+        return (both[:, :length] + both[:, length:]).reshape(GROUP, width, length)
+
+    local[6].wait()
+    origin = sdepth_v[...]
 
     def advance(t, z, old):
         own = pl.ds(REACH, width)
         v = field[t, pl.ds(REACH + z, GROUP), own, :]
-        total = (3.0 * CENTER) * v
+        total = (3.0 * CENTER) * v if ny > 1 else along(v)
         for k in range(1, REACH + 1):
             near = (
                 field[t, pl.ds(REACH + z + k, GROUP), own, :]
@@ -212,16 +246,14 @@
                 + field[t, pl.ds(REACH + z, GROUP), pl.ds(REACH - k, width), :]
             )
             total = total + COEFS[k - 1] * near
-            up = pltpu.roll(v, length - k, 2)
-            down = pltpu.roll(v, k, 2)
             if ny > 1:
+                up = pltpu.roll(v, length - k, 2)
+                down = pltpu.roll(v, k, 2)
                 low = pltpu.roll(side[t, 0, pl.ds(z, GROUP), :, :], k, 2)
                 high = pltpu.roll(side[t, 1, pl.ds(z, GROUP), :, :], length - k, 2)
                 up = jnp.where((lanes < length - k)[None], up, high)
                 down = jnp.where((lanes >= k)[None], down, low)
                 total = total + COEFS[k - 1] * (up + down)
-            else:
-                total = total + ahead[k - 1][None] * up + behind[k - 1][None] * down
         strength = courant_v[pl.ds(z, GROUP), :, :].astype(jnp.float32)
         levels = lax.broadcasted_iota(jnp.int32, (GROUP, width, length), 0) + z
         shot = jnp.where(levels == origin[None], amp[t][None], 0.0)
@@ -236,7 +268,7 @@
             field[1, pl.ds(REACH + z, GROUP), pl.ds(REACH, width), :] = new
             return inner
 
-        lax.fori_loop(0, rows // GROUP, group, 0)
+        lax.fori_loop(0, rows // GROUP, group, 0, unroll=True)
         send(1, c)
         return carry
 
@@ -254,7 +286,7 @@
             field[t + 1, pl.ds(REACH + z, GROUP), pl.ds(REACH, width), :] = new
             return inner
 
-        lax.fori_loop(0, rows // GROUP, group, 0)
+        lax.fori_loop(0, rows // GROUP, group, 0, unroll=True)
 
         @pl.when(t < STEPS - 1)
         def _():
@@ -270,7 +302,8 @@
     done.start()
 
     local[3].wait()
-    ground = rdepth[...]
+    local[7].wait()
+    ground = rdepth_v[...]
     product[pl.ds(0, 1), :, :] = jnp.zeros((1, width, length), jnp.float32)
     product[pl.ds(depth + 1, 1), :, :] = jnp.zeros((1, width, length), jnp.float32)
 
@@ -354,8 +387,6 @@
     ):
         depth, width, length = pressure.shape
         hbm = pl.BlockSpec(memory_space=pl.ANY)
-        vmem = pl.BlockSpec(memory_space=pltpu.VMEM)
-        smem = pl.BlockSpec(memory_space=pltpu.SMEM)
         flat = (depth, width, length)
         sides = (STEPS, 2, depth, width, length) if ny > 1 else (1, 1, 1, width, length)
         return pl.pallas_call(
@@ -364,7 +395,7 @@
                 jax.ShapeDtypeStruct(flat, jnp.float32),
                 jax.ShapeDtypeStruct((depth // nx, width * nx, length), jnp.float32),
             ),
-            in_specs=[hbm, hbm, hbm, smem, vmem, vmem, vmem, hbm],
+            in_specs=[hbm] * 8,
             out_specs=(hbm, hbm),
             scratch_shapes=[
                 pltpu.VMEM((STEPS + 1, depth + 2 * REACH, width + 2 * REACH, length), jnp.float32),
@@ -375,7 +406,12 @@
                 pltpu.VMEM((STEPS, width, length), jnp.float32),
                 pltpu.VMEM((depth + 2, width, length), jnp.float32),
                 pltpu.VMEM(flat, jnp.float32),
-                pltpu.SemaphoreType.DMA((4,)),
+                pltpu.VMEM((2 * length, 2 * length), jnp.bfloat16),
+                pltpu.SMEM(wavelet.shape, jnp.float32),
+                pltpu.VMEM((width, length), jnp.int32),
+                pltpu.VMEM((width, length), jnp.int32),
+                pltpu.VMEM((width, length), jnp.int32),
+                pltpu.SemaphoreType.DMA((8,)),
                 pltpu.SemaphoreType.DMA((STEPS, CHUNKS, 2)),
                 pltpu.SemaphoreType.DMA((STEPS, CHUNKS, 2)),
                 pltpu.SemaphoreType.DMA((STEPS, CHUNKS, 2)),
@@ -385,7 +421,7 @@
                 pltpu.SemaphoreType.DMA((nx,)),
             ],
             compiler_params=pltpu.CompilerParams(
-                collective_id=0, has_side_effects=True, vmem_limit_bytes=48 * 1024 * 1024
+                collective_id=0, has_side_effects=True, vmem_limit_bytes=67043328
             ),
         )(pressure, prior, courant, wavelet, delay, sdepth, rdepth, receiver)
 

time: 78.2 us -> 71.4 us (0.913)
  local copies, waits for them, and re-layouts: 8.37 us -> 2.72 us
  Pallas kernels: 68.8 us -> 67.9 us
    unnamed x18 -> x4, local copies, waits for them, and re-layouts: 8.37 us -> 2.72 us
    pallas_call x1, Pallas kernels: 68.8 us -> 67.9 us  [shards(): pl.pallas_call(functools.partial(kernel, nx, ny), out_shape=(jax.ShapeDty...]
where the time goes in v1:
time: 71.4 us; the launch traced here: 71.3 us
  Pallas kernels  67.9 us (95%)
  local copies, waits for them, and re-layouts  2.72 us (4%)
    pallas_call x1, Pallas kernels, shards(): pl.pallas_call(functools.partial(kernel, nx, ny), out_shape=(jax.ShapeDty...  67.9 us
    unnamed x4, local copies, waits for them, and re-layouts  2.72 us

profile of v1, /device:TPU:29, one launch (start us, length us, event | category | flops | bytes accessed | tf_op | source)
XLA Modules:
  0.0 71.3 jit_solution(16548025896012684032)
XLA Ops:
  0.6 67.9 %shard_map.95 = (f32[128,8,128]{2,1,0:T(8,128)}, f32[4,256,128]{2,1,0:T(8,128)}) custom-call(f32[128,8,128]{2,1,0:T(8,128)} %pressure.1, f32[128,8,128]{2,1,0:T(8,128)} %prior.1, bf16[128,8,128]{2,1,0:T(8,128)(2,1)} %courant.1, f32[16]{0:T(128)} %wavelet.1, s32[8,128]{1,0:T(8,128)} %delay.1, s32[8,128]{1,0:T(8,128)} %sdepth.1, s32[8,128]{1,0:T(8,128)} %rdepth.1, ...), custom_call_target="tpu_custom_call" | custom-call | tf_op jit(solution)/shard_map/pallas_call | solution.py:392
  68.5 0.0 copy-start
  68.5 1.9 %copy.12 = f32[128,8,128]{2,1,0:T(8,128)} copy(f32[128,8,128]{2,1,0:T(8,128)} %get-tuple-element.4) | data formatting | bytes 1048576
  70.5 0.0 copy-done
  70.5 0.8 %copy.13 = f32[4,256,128]{2,1,0:T(8,128)} copy(f32[4,256,128]{2,1,0:T(8,128)S(1)} %copy-done) | data formatting | bytes 1048576
Async XLA Ops:
  68.5 1.9 %copy-start = (f32[4,256,128]{2,1,0:T(8,128)S(1)}, f32[4,256,128]{2,1,0:T(8,128)}, u32[]{:S(2)}) copy-start(f32[4,256,128]{2,1,0:T(8,128)} %get-tuple-element.5) | copy-start | bytes 1572868

commit v2 on v1

--- a/solution.py
+++ b/solution.py
@@ -11,7 +11,7 @@
 REACH = 4
 CENTER = -205.0 / 72.0
 COEFS = (1.6, -0.2, 8.0 / 315.0, -1.0 / 560.0)
-CHUNKS = 4
+CHUNKS = 2
 GROUP = 8
 
 
@@ -49,6 +49,7 @@
     out_sem,
     img_send,
     img_recv,
+    known,
 ):
     depth, width, length = pressure.shape
     rows = depth // CHUNKS
@@ -72,7 +73,8 @@
         copy.start()
 
     barrier = pltpu.get_barrier_semaphore()
-    for j in range(1, nx):
+    beside = sorted({1, nx - 1} - {0}) if nx > 1 else []
+    for j in beside:
         pl.semaphore_signal(
             barrier,
             inc=1,
@@ -141,8 +143,8 @@
             total = total + jnp.where(late + t == pick, wave_v[pick], 0.0)
         amp[t] = total
 
-    if nx + ny > 2:
-        pl.semaphore_wait(barrier, nx + ny - 2)
+    if len(beside) + ny > 1:
+        pl.semaphore_wait(barrier, len(beside) + ny - 1)
 
     def span(c):
         return pl.ds(REACH + c * rows, rows)
@@ -274,9 +276,38 @@
 
     lax.fori_loop(0, CHUNKS, first_chunk, 0)
 
+    reach = []
+    while (reach[-1] * 2 if reach else 1) < nx // 2:
+        reach.append(reach[-1] * 2 if reach else 1)
+
+    def greet(number):
+        for way, j in enumerate((reach[number], nx - reach[number])):
+            pl.semaphore_signal(
+                known.at[number, way],
+                inc=1,
+                device_id={"gx": lax.rem(me + j, nx)},
+                device_id_type=pl.DeviceIdType.MESH,
+            )
+
+    def greeted(number):
+        for way in (0, 1):
+            pl.semaphore_wait(known.at[number, way], 1)
+
+    def meet(number):
+        if number > 0:
+            greeted(number - 1)
+        greet(number)
+
     def step(i, carry):
         t = i // CHUNKS
         c = i % CHUNKS
+        for number in range(len(reach)):
+            if CHUNKS + 3 * number < STEPS * CHUNKS:
+
+                @pl.when(i == CHUNKS + 3 * number)
+                def _():
+                    meet(number)
+
         arrived(t, c)
 
         def group(g, inner):
@@ -295,6 +326,11 @@
         return carry
 
     lax.fori_loop(CHUNKS, STEPS * CHUNKS, step, 0)
+    for number in range(len(reach)):
+        if CHUNKS + 3 * number >= STEPS * CHUNKS:
+            meet(number)
+    if reach:
+        greeted(len(reach) - 1)
 
     done = pltpu.make_async_copy(
         field.at[STEPS, pl.ds(REACH, depth), pl.ds(REACH, width), :], final, out_sem.at[0]
@@ -419,6 +455,7 @@
                 pltpu.SemaphoreType.DMA((2,)),
                 pltpu.SemaphoreType.DMA((nx,)),
                 pltpu.SemaphoreType.DMA((nx,)),
+                pltpu.SemaphoreType.REGULAR((max(nx.bit_length(), 1), 2)),
             ],
             compiler_params=pltpu.CompilerParams(
                 collective_id=0, has_side_effects=True, vmem_limit_bytes=67043328

time: 71.4 us -> 69.8 us (0.978)
  Pallas kernels: 67.9 us -> 66.2 us
    pallas_call x1, Pallas kernels: 67.9 us -> 66.2 us  [shards(): pl.pallas_call(functools.partial(kernel, nx, ny), out_shape=(jax.ShapeDty...]
where the time goes in v2:
time: 69.8 us; the launch traced here: 69.6 us
  Pallas kernels  66.2 us (95%)
  local copies, waits for them, and re-layouts  2.72 us (4%)
    pallas_call x1, Pallas kernels, shards(): pl.pallas_call(functools.partial(kernel, nx, ny), out_shape=(jax.ShapeDty...  66.2 us
    unnamed x4, local copies, waits for them, and re-layouts  2.72 us

profile of v2, /device:TPU:29, one launch (start us, length us, event | category | flops | bytes accessed | tf_op | source)
XLA Modules:
  0.0 69.6 jit_solution(1266980511837446637)
XLA Ops:
  0.6 66.2 %shard_map.95 = (f32[128,8,128]{2,1,0:T(8,128)}, f32[4,256,128]{2,1,0:T(8,128)}) custom-call(f32[128,8,128]{2,1,0:T(8,128)} %pressure.1, f32[128,8,128]{2,1,0:T(8,128)} %prior.1, bf16[128,8,128]{2,1,0:T(8,128)(2,1)} %courant.1, f32[16]{0:T(128)} %wavelet.1, s32[8,128]{1,0:T(8,128)} %delay.1, s32[8,128]{1,0:T(8,128)} %sdepth.1, s32[8,128]{1,0:T(8,128)} %rdepth.1, ...), custom_call_target="tpu_custom_call" | custom-call | tf_op jit(solution)/shard_map/pallas_call | solution.py:428
  66.9 0.0 copy-start
  66.9 1.9 %copy.12 = f32[128,8,128]{2,1,0:T(8,128)} copy(f32[128,8,128]{2,1,0:T(8,128)} %get-tuple-element.4) | data formatting | bytes 1048576
  68.8 0.0 copy-done
  68.8 0.8 %copy.13 = f32[4,256,128]{2,1,0:T(8,128)} copy(f32[4,256,128]{2,1,0:T(8,128)S(1)} %copy-done) | data formatting | bytes 1048576
Async XLA Ops:
  66.9 1.9 %copy-start = (f32[4,256,128]{2,1,0:T(8,128)S(1)}, f32[4,256,128]{2,1,0:T(8,128)}, u32[]{:S(2)}) copy-start(f32[4,256,128]{2,1,0:T(8,128)} %get-tuple-element.5) | copy-start | bytes 1572868
